TPU v7x, 256 devices: a 8x8x2 block of a 8x8x16 slice. The times are simulated.
256 devices in a mesh: groups: 2 (over z), expert: 16 (over x, core), tensor: 8 (over y).
Axes of the slice: x: 8, y: 8, z: 2, core: 2. Of those that a mesh axis runs over, the one named last changes fastest.
The devices are a block of a 8x8x16 slice.
Arguments:
- tokens: bfloat16 [2048, 4096], P(('groups', 'expert'), 'tensor'), parts along dimension 0, may hold values from -400 to 400
- norm_gain: float32 [4096], replicated, may hold values from 0.5 to 1.5
- w_gate: bfloat16 [4096, 65536], P(None, ('expert', 'tensor')), may hold values from -0.09375 to 0.09375
- w_up: bfloat16 [4096, 65536], P(None, ('expert', 'tensor')), may hold values from -0.09375 to 0.09375
- w_down: bfloat16 [65536, 4096], P(('expert', 'tensor')), may hold values from -0.0625 to 0.0625
- expert_ids: int32 [2048, 2], P(('groups', 'expert')), parts along dimension 0, may hold values from 0 to 7, all different within a row; in each aligned block of 64 rows (0 to 63, 64 to 127, ...) at most 32 rows name the same one
- gate_weights: float32 [2048, 2], P(('groups', 'expert')), parts along dimension 0, may hold values from 0.1 to 1
Outputs:
- moe_out: bfloat16 [2048, 4096], P(('groups', 'expert'), 'tensor'), parts along dimension 0
There are 2 independent parts, one for each index of `groups`. A program takes and returns all parts, laid end to end along the dimension named above; an argument that names none is the same for every part. Nothing has to cross between parts.
Inputs may be any that keep to these rules, and one draw needn't show every extreme that they name: `expert_ids`: each request names two different experts. Within the rows of one device (aligned blocks of 64 rows) no expert is named by more than 32 rows, and in some blocks one expert is named by exactly 32 rows.
All inputs are finite; a program needn't handle non-finite values.
Results may differ from a plain program's by a relative error of at most 0.008.
Values may be sent and summed in bfloat16 or wider, within the bound.
No kernel may reach another device: no remote copies, remote signals or barrier semaphores. Data moves between devices by JAX's collectives and lax.ppermute only.
A program may use at most 128 MiB of HBM per device.

v0:
```python
import jax
import jax.numpy as jnp
from jax import lax
from jax.experimental import pallas as pl
from jax.experimental.pallas import tpu as pltpu
from jax.sharding import Mesh, PartitionSpec as P


EXPERTS = 8
CHUNKS = 1


def shift(value, axis, by):
    size = lax.axis_size(axis)
    return lax.ppermute(value, axis, [(i, (i + by) % size) for i in range(size)])


def hold_on_chip(*arrays):
    def kernel(*refs):
        count = len(arrays)
        sources, targets, done = refs[:count], refs[count : 2 * count], refs[2 * count]
        copies = [
            pltpu.make_async_copy(sources[k], targets[k], done.at[k]) for k in range(count)
        ]
        for copy in copies:
            copy.start()
        for copy in copies:
            copy.wait()

    return pl.pallas_call(
        kernel,
        out_shape=[pltpu.VMEM(a.shape, a.dtype) for a in arrays],
        in_specs=[pl.BlockSpec(memory_space=pl.ANY) for _ in arrays],
        out_specs=[pl.BlockSpec(memory_space=pltpu.VMEM) for _ in arrays],
        scratch_shapes=[pltpu.SemaphoreType.DMA((len(arrays),))],
        compiler_params=pltpu.CompilerParams(vmem_limit_bytes=1 << 20),
    )(*arrays)


def block_of(value, index, size, axis):
    return lax.dynamic_slice_in_dim(value, index * size, size, axis)


def gather_features(chunks, use):
    n = lax.axis_size("tensor")
    me = lax.axis_index("tensor")
    right, left = list(chunks), list(chunks)
    for i, chunk in enumerate(chunks):
        use(i, chunk, me)
    for step in range(1, n // 2 + 1):
        for i in range(len(chunks)):
            right[i] = shift(right[i], "tensor", 1)
            if step < n - n // 2:
                left[i] = shift(left[i], "tensor", -1)
            use(i, right[i], (me - step) % n)
            if step < n - n // 2:
                use(i, left[i], (me + step) % n)


def sum_features(make, count):
    n = lax.axis_size("tensor")
    me = lax.axis_index("tensor")
    right, left = [None] * count, [None] * count
    far = n // 2
    for step in range(far):
        for i in range(count):
            value = make(i, (me + far - step) % n)
            if right[i] is not None:
                value = value + right[i].astype(jnp.float32)
            right[i] = shift(value.astype(jnp.bfloat16), "tensor", 1)
            if step < n - 1 - far:
                value = make(i, (me - (n - 1 - far - step)) % n)
                if left[i] is not None:
                    value = value + left[i].astype(jnp.float32)
                left[i] = shift(value.astype(jnp.bfloat16), "tensor", -1)
    return [
        make(i, me) + right[i].astype(jnp.float32) + left[i].astype(jnp.float32)
        for i in range(count)
    ]


def per_device(tokens, norm_gain, w_gate, w_up, w_down, expert_ids, gate_weights):
    columns, halves = lax.axis_size("column"), lax.axis_size("half")
    tok_rows, w = tokens.shape
    width = w * lax.axis_size("tensor")
    slots = tok_rows // 2
    share = slots // halves
    f32, bf16 = jnp.float32, jnp.bfloat16

    def swap(value):
        return [value] + [shift(value, "half", k) for k in range(1, halves)]

    gates, ups, downs = swap(w_gate), swap(w_up), swap(w_down)
    for k in range(1, halves):
        gates[k], ups[k], downs[k] = hold_on_chip(gates[k], ups[k], downs[k])

    experts = jnp.arange(EXPERTS, dtype=jnp.int32)
    hits = (expert_ids[:, :, None] == experts[None, None, :]).astype(f32)
    chosen = jnp.sum(hits, axis=1)
    order = jnp.arange(tok_rows, dtype=jnp.int32)
    earlier = (order[:, None] > order[None, :]).astype(bf16)
    rank = jnp.dot(earlier, chosen.astype(bf16), preferred_element_type=f32)
    slot = jnp.arange(slots, dtype=jnp.int32).astype(f32)
    select = chosen.T[:, None, :] * (rank.T[:, None, :] == slot[None, :, None]).astype(f32)
    weight = jnp.sum(hits * gate_weights[:, :, None], axis=1)

    pick = select.reshape(EXPERTS * slots, tok_rows).astype(bf16)
    packed = jnp.dot(pick, tokens, preferred_element_type=f32).astype(bf16)
    packed = packed.reshape(columns * halves, share, w)

    def exchange(value):
        return lax.all_to_all(value, ("column", "half"), 0, 0, tiled=True)

    arrived = exchange(packed).reshape(columns * halves * share, w)
    rows = arrived.shape[0] // CHUNKS
    gate_sums = [[0.0] * halves for _ in range(CHUNKS)]
    up_sums = [[0.0] * halves for _ in range(CHUNKS)]
    squares = [0.0] * CHUNKS

    def accumulate(i, block, owner):
        values = block.astype(f32)
        squares[i] = squares[i] + jnp.sum(values * values, axis=1, keepdims=True)
        scaled = (values * block_of(norm_gain, owner, w, 0)[None, :]).astype(bf16)
        for k in range(halves):
            gate, up = block_of(gates[k], owner, w, 0), block_of(ups[k], owner, w, 0)
            gate_sums[i][k] = gate_sums[i][k] + jnp.dot(scaled, gate, preferred_element_type=f32)
            up_sums[i][k] = up_sums[i][k] + jnp.dot(scaled, up, preferred_element_type=f32)

    gather_features([arrived[i * rows : (i + 1) * rows] for i in range(CHUNKS)], accumulate)
    hidden = []
    for i in range(CHUNKS):
        scale = lax.rsqrt(squares[i] / width + 1e-05)
        hidden.append(
            [
                (jax.nn.silu(g * scale) * (u * scale)).astype(bf16)
                for g, u in zip(gate_sums[i], up_sums[i])
            ]
        )

    def partial(i, owner):
        return sum(
            jnp.dot(h, block_of(down, owner, w, 1), preferred_element_type=f32)
            for h, down in zip(hidden[i], downs)
        )

    summed = sum_features(partial, CHUNKS)
    summed = jnp.concatenate(summed, axis=0).astype(bf16)
    returned = exchange(summed.reshape(columns * halves, share, w))
    returned = returned.reshape(EXPERTS * slots, w)
    mix = (select * weight.T[:, None, :]).reshape(EXPERTS * slots, tok_rows)
    mixed = lax.dot_general(
        mix,
        returned.astype(f32),
        (((0,), (0,)), ((), ())),
        precision=lax.Precision.HIGHEST,
        preferred_element_type=f32,
    )
    return mixed.astype(bf16)


def solution(mesh):
    groups, n_expert, n_tensor = (mesh.shape[a] for a in ("groups", "expert", "tensor"))
    halves = n_expert // EXPERTS
    inner = Mesh(
        mesh.devices.reshape(groups, EXPERTS, halves, n_tensor),
        ("groups", "column", "half", "tensor"),
    )
    rows = ("groups", "column", "half")
    hidden = ("column", "half", "tensor")
    in_specs = (
        P(rows, "tensor"),
        P(),
        P(None, hidden),
        P(None, hidden),
        P(hidden, None),
        P(rows, None),
        P(rows, None),
    )

    return jax.shard_map(
        per_device, mesh=inner, in_specs=in_specs, out_specs=P(rows, "tensor"), check_vma=False
    )
```

profile of v0, /device:TPU:513, one launch (start us, length us, event | category | flops | bytes accessed | tf_op | source)
XLA Modules:
  0.0 141.0 jit_solution(6688164634304354311)
XLA Ops:
  0.0 0.7 convert_reduce_fusion
  1.1 0.9 convolution_convert_fusion
  2.0 23.7 %all-to-all-start = ((bf16[16,16,512]{2,1,0:T(8,128)(2,1)}), bf16[16,16,512]{2,1,0:T(8,128)(2,1)S(1)}, u32[]{:S(2)}, u32[]{:S(2)}) async-start(bf16[16,16,512]{2,1,0:T(8,128)(2,1)} %bitcast.5), calls=%async_computation | async-start | bytes 524288 | tf_op jit(solution)/shard_map/all_to_all | solution.py:112
  25.7 0.8 collective-permute-start.7
  26.7 0.4 collective-permute-start.9
  27.0 0.9 fusion.196
  27.9 9.8 %all-to-all-done = bf16[16,16,512]{2,1,0:T(8,128)(2,1)S(1)} async-done(((bf16[16,16,512]{2,1,0:T(8,128)(2,1)}), bf16[16,16,512]{2,1,0:T(8,128)(2,1)S(1)}, u32[]{:S(2)}, u32[]{:S(2)}) %all-to-all-start) | async-done | bytes 262176 | tf_op jit(solution)/shard_map/all_to_all | solution.py:112
  37.7 1.5 %collective-permute-start = (bf16[256,512]{1,0:T(8,128)(2,1)S(1)}, bf16[256,512]{1,0:T(8,128)(2,1)S(1)}, u32[]{:S(2)}, u32[]{:S(2)}) collective-permute-start(bf16[256,512]{1,0:T(8,128)(2,1)S(1)} %bitcast.36), channel_id=1, source_target_pairs={{0,1},{1,2},{2,3},{3,4},{4,5},{5,6},{6,7},{7,0},{8,9},{9,10},{10,1... | collective-permute-start | bytes 786440 | tf_op jit(solution)/shard_map/ppermute | solution.py:15
  39.2 1.3 fusion.115
  40.7 1.5 %fusion.104 = f32[256,512]{1,0:T(8,128)S(1)} fusion(bf16[4096,512]{1,0:T(8,128)(2,1)} %param.10, s32[]{:T(128)S(6)} %select_n.121, bf16[256,512]{1,0:T(8,128)(2,1)S(1)} %bitcast.38, f32[512]{0:T(512)S(1)} %get-tuple-element.19), kind=kOutput, calls=%fused_computation.146 | convolution fusion | flops 134610944 | bytes 1312772 | tf_op jit(solution)/shard_map/dot_general | solution.py:127
  42.2 4.5 %collective-permute-done = bf16[256,512]{1,0:T(8,128)(2,1)S(1)} collective-permute-done((bf16[256,512]{1,0:T(8,128)(2,1)S(1)}, bf16[256,512]{1,0:T(8,128)(2,1)S(1)}, u32[]{:S(2)}, u32[]{:S(2)}) %collective-permute-start) | collective-permute-done | bytes 262176 | tf_op jit(solution)/shard_map/ppermute | solution.py:15
  46.7 0.8 collective-permute-start.2
  47.6 2.0 %collective-permute-start.3 = (bf16[256,512]{1,0:T(8,128)(2,1)S(1)}, bf16[256,512]{1,0:T(8,128)(2,1)S(1)}, u32[]{:S(2)}, u32[]{:S(2)}) collective-permute-start(bf16[256,512]{1,0:T(8,128)(2,1)S(1)} %collective-permute-done.1), channel_id=1, source_target_pairs={{0,7},{1,0},{2,1},{3,2},{4,3},{5,4},{6,5},{7,6},{8,15},{9,8},{10,9... | collective-permute-start | bytes 786440 | tf_op jit(solution)/shard_map/ppermute | solution.py:15
  49.6 1.5 %convolution_add_fusion.25 = f32[256,512]{1,0:T(8,128)S(1)} fusion(f32[256,512]{1,0:T(8,128)S(1)} %fusion.115, bf16[4096,512]{1,0:T(8,128)(2,1)} %param.9, s32[]{:T(128)S(6)} %select_n.123, bf16[256,512]{1,0:T(8,128)(2,1)S(1)} %collective-permute-done, f32[512]{0:T(512)S(1)} %get-tuple-element.18), kind=kOutput, calls=%fused_computation.48 | convolution fusion | flops 134742016 | bytes 1837060 | tf_op jit(solution)/shard_map/dot_general | solution.py:126
  51.1 1.3 convolution_add_fusion.20
  52.5 0.3 convolution_add_fusion.24
  53.0 1.4 convolution_add_fusion.19
  54.3 0.6 collective-permute-done.3
  54.9 3.1 %collective-permute-start.5 = (bf16[256,512]{1,0:T(8,128)(2,1)S(1)}, bf16[256,512]{1,0:T(8,128)(2,1)S(1)}, u32[]{:S(2)}, u32[]{:S(2)}) collective-permute-start(bf16[256,512]{1,0:T(8,128)(2,1)S(1)} %collective-permute-done.3), channel_id=1, source_target_pairs={{0,7},{1,0},{2,1},{3,2},{4,3},{5,4},{6,5},{7,6},{8,15},{9,8},{10,9... | collective-permute-start | bytes 786440 | tf_op jit(solution)/shard_map/ppermute | solution.py:15
  58.0 0.3 fusion.110
  58.7 0.3 fusion.22
  59.0 0.3 fusion.19
  59.6 5.7 %collective-permute-done.4 = bf16[256,512]{1,0:T(8,128)(2,1)S(1)} collective-permute-done((bf16[256,512]{1,0:T(8,128)(2,1)S(1)}, bf16[256,512]{1,0:T(8,128)(2,1)S(1)}, u32[]{:S(2)}, u32[]{:S(2)}) %collective-permute-start.4) | collective-permute-done | bytes 262176 | tf_op jit(solution)/shard_map/ppermute | solution.py:15
  66.2 0.3 fusion.21
  66.6 0.3 fusion.18
  66.9 4.8 %collective-permute-done.6 = bf16[256,512]{1,0:T(8,128)(2,1)S(1)} collective-permute-done((bf16[256,512]{1,0:T(8,128)(2,1)S(1)}, bf16[256,512]{1,0:T(8,128)(2,1)S(1)}, u32[]{:S(2)}, u32[]{:S(2)}) %collective-permute-start.6) | collective-permute-done | bytes 262176 | tf_op jit(solution)/shard_map/ppermute | solution.py:15
  71.9 0.3 fusion.20
  72.2 0.4 fusion.28
  72.6 0.3 fusion.60
  72.9 0.3 fusion.63
  73.2 0.3 fusion.66
  73.6 0.3 fusion.57
  73.9 4.7 %shard_map.73 = (bf16[4096,512]{1,0:T(8,128)(2,1)S(1)}, bf16[4096,512]{1,0:T(8,128)(2,1)S(1)}, bf16[512,4096]{1,0:T(8,128)(2,1)S(1)}) custom-call(bf16[4096,512]{1,0:T(8,128)(2,1)} %collective-permute-done.7.refs_0_, bf16[4096,512]{1,0:T(8,128)(2,1)} %collective-permute-done.8.refs_1_, bf16[512,4096]{1,0:T(8,128)(2,1)} %collective-permute-done.9.refs_2_), custom_call_target="tpu_custom_call" | custom-call | tf_op jit(solution)/shard_map/pallas_call | solution.py:30
  78.6 0.3 fusion.88
  78.9 0.3 fusion.90
  79.2 0.3 fusion.15
  79.6 0.3 fusion.76
  79.9 0.3 fusion.78
  80.2 0.3 fusion.11
  81.8 0.3 fusion.14
  82.1 0.3 fusion.13
  82.4 0.3 fusion.12
  82.8 0.3 fusion.10
  83.1 0.3 fusion.9
  83.4 0.4 fusion.29
  83.8 0.3 fusion.31
  84.3 0.3 fusion.48
  84.6 0.3 fusion.32
  84.9 2.8 %collective-permute-start.14 = (bf16[256,512]{1,0:T(8,128)(2,1)S(1)}, bf16[256,512]{1,0:T(8,128)(2,1)S(1)}, u32[]{:S(2)}, u32[]{:S(2)}) collective-permute-start(bf16[256,512]{1,0:T(8,128)(2,1)S(1)} %fusion.32), channel_id=1, source_target_pairs={{0,7},{1,0},{2,1},{3,2},{4,3},{5,4},{6,5},{7,6},{8,15},{9,8},{10,9... | collective-permute-start | bytes 786440 | tf_op jit(solution)/shard_map/ppermute | solution.py:15
  87.6 3.0 %collective-permute-done.10 = bf16[256,512]{1,0:T(8,128)(2,1)S(1)} collective-permute-done((bf16[256,512]{1,0:T(8,128)(2,1)S(1)}, bf16[256,512]{1,0:T(8,128)(2,1)S(1)}, u32[]{:S(2)}, u32[]{:S(2)}) %collective-permute-start.10) | collective-permute-done | bytes 262176 | tf_op jit(solution)/shard_map/ppermute | solution.py:15
  91.1 0.3 fusion.51
  91.4 0.3 fusion.27
  91.8 2.8 %collective-permute-start.15 = (bf16[256,512]{1,0:T(8,128)(2,1)S(1)}, bf16[256,512]{1,0:T(8,128)(2,1)S(1)}, u32[]{:S(2)}, u32[]{:S(2)}) collective-permute-start(bf16[256,512]{1,0:T(8,128)(2,1)S(1)} %fusion.27), channel_id=1, source_target_pairs={{0,7},{1,0},{2,1},{3,2},{4,3},{5,4},{6,5},{7,6},{8,15},{9,8},{10,9... | collective-permute-start | bytes 786440 | tf_op jit(solution)/shard_map/ppermute | solution.py:15
  94.5 3.2 %collective-permute-done.11 = bf16[256,512]{1,0:T(8,128)(2,1)S(1)} collective-permute-done((bf16[256,512]{1,0:T(8,128)(2,1)S(1)}, bf16[256,512]{1,0:T(8,128)(2,1)S(1)}, u32[]{:S(2)}, u32[]{:S(2)}) %collective-permute-start.11) | collective-permute-done | bytes 262176 | tf_op jit(solution)/shard_map/ppermute | solution.py:15
  98.2 0.3 fusion.54
  98.5 0.3 fusion.26
  98.8 3.0 %collective-permute-start.16 = (bf16[256,512]{1,0:T(8,128)(2,1)S(1)}, bf16[256,512]{1,0:T(8,128)(2,1)S(1)}, u32[]{:S(2)}, u32[]{:S(2)}) collective-permute-start(bf16[256,512]{1,0:T(8,128)(2,1)S(1)} %fusion.26), channel_id=1, source_target_pairs={{0,7},{1,0},{2,1},{3,2},{4,3},{5,4},{6,5},{7,6},{8,15},{9,8},{10,9... | collective-permute-start | bytes 786440 | tf_op jit(solution)/shard_map/ppermute | solution.py:15
  101.9 4.1 %collective-permute-done.12 = bf16[256,512]{1,0:T(8,128)(2,1)S(1)} collective-permute-done((bf16[256,512]{1,0:T(8,128)(2,1)S(1)}, bf16[256,512]{1,0:T(8,128)(2,1)S(1)}, u32[]{:S(2)}, u32[]{:S(2)}) %collective-permute-start.12) | collective-permute-done | bytes 262176 | tf_op jit(solution)/shard_map/ppermute | solution.py:15
  106.4 0.3 fusion.93
  106.8 8.5 %collective-permute-done.13 = bf16[256,512]{1,0:T(8,128)(2,1)S(1)} collective-permute-done((bf16[256,512]{1,0:T(8,128)(2,1)S(1)}, bf16[256,512]{1,0:T(8,128)(2,1)S(1)}, u32[]{:S(2)}, u32[]{:S(2)}) %collective-permute-start.13) | collective-permute-done | bytes 262176 | tf_op jit(solution)/shard_map/ppermute | solution.py:15
  115.3 1.0 fusion.30
  116.4 11.7 %all-to-all-start.1 = ((bf16[16,16,512]{2,1,0:T(8,128)(2,1)}), bf16[16,16,512]{2,1,0:T(8,128)(2,1)S(1)}, u32[]{:S(2)}, u32[]{:S(2)}) async-start(bf16[16,16,512]{2,1,0:T(8,128)(2,1)} %bitcast.7), calls=%async_computation.1 | async-start | bytes 524288 | tf_op jit(solution)/shard_map/all_to_all | solution.py:112
  128.2 11.9 %all-to-all-done.1 = bf16[16,16,512]{2,1,0:T(8,128)(2,1)S(1)} async-done(((bf16[16,16,512]{2,1,0:T(8,128)(2,1)}), bf16[16,16,512]{2,1,0:T(8,128)(2,1)S(1)}, u32[]{:S(2)}, u32[]{:S(2)}) %all-to-all-start.1) | async-done | bytes 262176 | tf_op jit(solution)/shard_map/all_to_all | solution.py:112
  140.1 0.9 convolution_convert_fusion.1
  (51 shorter events, 5.4 us)
Async XLA Ops:
  0.0 1.1 copy-start
  2.0 35.7 %all-to-all-start = ((bf16[16,16,512]{2,1,0:T(8,128)(2,1)}), bf16[16,16,512]{2,1,0:T(8,128)(2,1)S(1)}, u32[]{:S(2)}, u32[]{:S(2)}) async-start(bf16[16,16,512]{2,1,0:T(8,128)(2,1)} %bitcast.5), calls=%async_computation | async-start | bytes 524288 | tf_op jit(solution)/shard_map/all_to_all | solution.py:112
  25.7 48.1 %collective-permute-start.7 = (bf16[4096,512]{1,0:T(8,128)(2,1)}, bf16[4096,512]{1,0:T(8,128)(2,1)}, u32[]{:S(2)}, u32[]{:S(2)}) collective-permute-start(bf16[4096,512]{1,0:T(8,128)(2,1)} %param.9), channel_id=1, source_target_pairs={{0,8},{8,0},{1,9},{9,1},{2,10},{10,2},{3,11},{11,3},{4,12},{12,4},... | collective-permute-start | bytes 12582920 | tf_op jit(solution)/shard_map/ppermute | solution.py:15
  26.5 47.4 %collective-permute-start.8 = (bf16[4096,512]{1,0:T(8,128)(2,1)}, bf16[4096,512]{1,0:T(8,128)(2,1)}, u32[]{:S(2)}, u32[]{:S(2)}) collective-permute-start(bf16[4096,512]{1,0:T(8,128)(2,1)} %param.10), channel_id=1, source_target_pairs={{0,8},{8,0},{1,9},{9,1},{2,10},{10,2},{3,11},{11,3},{4,12},{12,4},... | collective-permute-start | bytes 12582920 | tf_op jit(solution)/shard_map/ppermute | solution.py:15
  26.7 47.2 %collective-permute-start.9 = (bf16[512,4096]{1,0:T(8,128)(2,1)}, bf16[512,4096]{1,0:T(8,128)(2,1)}, u32[]{:S(2)}, u32[]{:S(2)}) collective-permute-start(bf16[512,4096]{1,0:T(8,128)(2,1)} %param.11), channel_id=1, source_target_pairs={{0,8},{8,0},{1,9},{9,1},{2,10},{10,2},{3,11},{11,3},{4,12},{12,4},... | collective-permute-start | bytes 12582920 | tf_op jit(solution)/shard_map/ppermute | solution.py:15
  37.7 9.9 %collective-permute-start.1 = (bf16[256,512]{1,0:T(8,128)(2,1)S(1)}, bf16[256,512]{1,0:T(8,128)(2,1)S(1)}, u32[]{:S(2)}, u32[]{:S(2)}) collective-permute-start(bf16[256,512]{1,0:T(8,128)(2,1)S(1)} %bitcast.35), channel_id=1, source_target_pairs={{0,7},{1,0},{2,1},{3,2},{4,3},{5,4},{6,5},{7,6},{8,15},{9,8},{10,9... | collective-permute-start | bytes 786440 | tf_op jit(solution)/shard_map/ppermute | solution.py:15
  37.7 9.0 %collective-permute-start = (bf16[256,512]{1,0:T(8,128)(2,1)S(1)}, bf16[256,512]{1,0:T(8,128)(2,1)S(1)}, u32[]{:S(2)}, u32[]{:S(2)}) collective-permute-start(bf16[256,512]{1,0:T(8,128)(2,1)S(1)} %bitcast.36), channel_id=1, source_target_pairs={{0,1},{1,2},{2,3},{3,4},{4,5},{5,6},{6,7},{7,0},{8,9},{9,10},{10,1... | collective-permute-start | bytes 786440 | tf_op jit(solution)/shard_map/ppermute | solution.py:15
  40.7 11.8 %copy-start.2 = (bf16[4096,512]{1,0:T(8,128)(2,1)S(1)}, bf16[4096,512]{1,0:T(8,128)(2,1)}, u32[]{:S(2)}) copy-start(bf16[4096,512]{1,0:T(8,128)(2,1)} %param.9) | copy-start | bytes 12582916
  46.7 11.3 %collective-permute-start.2 = (bf16[256,512]{1,0:T(8,128)(2,1)S(1)}, bf16[256,512]{1,0:T(8,128)(2,1)S(1)}, u32[]{:S(2)}, u32[]{:S(2)}) collective-permute-start(bf16[256,512]{1,0:T(8,128)(2,1)S(1)} %collective-permute-done), channel_id=1, source_target_pairs={{0,1},{1,2},{2,3},{3,4},{4,5},{5,6},{6,7},{7,0},{8,9},{9,10},{10,1... | collective-permute-start | bytes 786440 | tf_op jit(solution)/shard_map/ppermute | solution.py:15
  47.6 7.3 %collective-permute-start.3 = (bf16[256,512]{1,0:T(8,128)(2,1)S(1)}, bf16[256,512]{1,0:T(8,128)(2,1)S(1)}, u32[]{:S(2)}, u32[]{:S(2)}) collective-permute-start(bf16[256,512]{1,0:T(8,128)(2,1)S(1)} %collective-permute-done.1), channel_id=1, source_target_pairs={{0,7},{1,0},{2,1},{3,2},{4,3},{5,4},{6,5},{7,6},{8,15},{9,8},{10,9... | collective-permute-start | bytes 786440 | tf_op jit(solution)/shard_map/ppermute | solution.py:15
  49.6 8.7 %copy-start.3 = (bf16[4096,512]{1,0:T(8,128)(2,1)S(1)}, bf16[4096,512]{1,0:T(8,128)(2,1)}, u32[]{:S(2)}) copy-start(bf16[4096,512]{1,0:T(8,128)(2,1)} %param.10) | copy-start | bytes 12582916
  54.9 10.5 %collective-permute-start.5 = (bf16[256,512]{1,0:T(8,128)(2,1)S(1)}, bf16[256,512]{1,0:T(8,128)(2,1)S(1)}, u32[]{:S(2)}, u32[]{:S(2)}) collective-permute-start(bf16[256,512]{1,0:T(8,128)(2,1)S(1)} %collective-permute-done.3), channel_id=1, source_target_pairs={{0,7},{1,0},{2,1},{3,2},{4,3},{5,4},{6,5},{7,6},{8,15},{9,8},{10,9... | collective-permute-start | bytes 786440 | tf_op jit(solution)/shard_map/ppermute | solution.py:15
  58.0 7.3 %collective-permute-start.4 = (bf16[256,512]{1,0:T(8,128)(2,1)S(1)}, bf16[256,512]{1,0:T(8,128)(2,1)S(1)}, u32[]{:S(2)}, u32[]{:S(2)}) collective-permute-start(bf16[256,512]{1,0:T(8,128)(2,1)S(1)} %collective-permute-done.2), channel_id=1, source_target_pairs={{0,1},{1,2},{2,3},{3,4},{4,5},{5,6},{6,7},{7,0},{8,9},{9,10},{10,1... | collective-permute-start | bytes 786440 | tf_op jit(solution)/shard_map/ppermute | solution.py:15
  65.3 6.4 %collective-permute-start.6 = (bf16[256,512]{1,0:T(8,128)(2,1)S(1)}, bf16[256,512]{1,0:T(8,128)(2,1)S(1)}, u32[]{:S(2)}, u32[]{:S(2)}) collective-permute-start(bf16[256,512]{1,0:T(8,128)(2,1)S(1)} %collective-permute-done.4), channel_id=1, source_target_pairs={{0,1},{1,2},{2,3},{3,4},{4,5},{5,6},{6,7},{7,0},{8,9},{9,10},{10,1... | collective-permute-start | bytes 786440 | tf_op jit(solution)/shard_map/ppermute | solution.py:15
  66.6 6.1 %copy-start.1 = (bf16[512,4096]{1,0:T(8,128)(2,1)S(1)}, bf16[512,4096]{1,0:T(8,128)(2,1)}, u32[]{:S(2)}) copy-start(bf16[512,4096]{1,0:T(8,128)(2,1)} %param.11) | copy-start | bytes 12582916
  84.1 6.5 %collective-permute-start.10 = (bf16[256,512]{1,0:T(8,128)(2,1)S(1)}, bf16[256,512]{1,0:T(8,128)(2,1)S(1)}, u32[]{:S(2)}, u32[]{:S(2)}) collective-permute-start(bf16[256,512]{1,0:T(8,128)(2,1)S(1)} %fusion.31), channel_id=1, source_target_pairs={{0,1},{1,2},{2,3},{3,4},{4,5},{5,6},{6,7},{7,0},{8,9},{9,10},{10,1... | collective-permute-start | bytes 786440 | tf_op jit(solution)/shard_map/ppermute | solution.py:15
  84.9 6.5 %collective-permute-start.14 = (bf16[256,512]{1,0:T(8,128)(2,1)S(1)}, bf16[256,512]{1,0:T(8,128)(2,1)S(1)}, u32[]{:S(2)}, u32[]{:S(2)}) collective-permute-start(bf16[256,512]{1,0:T(8,128)(2,1)S(1)} %fusion.32), channel_id=1, source_target_pairs={{0,7},{1,0},{2,1},{3,2},{4,3},{5,4},{6,5},{7,6},{8,15},{9,8},{10,9... | collective-permute-start | bytes 786440 | tf_op jit(solution)/shard_map/ppermute | solution.py:15
  91.0 6.8 %collective-permute-start.11 = (bf16[256,512]{1,0:T(8,128)(2,1)S(1)}, bf16[256,512]{1,0:T(8,128)(2,1)S(1)}, u32[]{:S(2)}, u32[]{:S(2)}) collective-permute-start(bf16[256,512]{1,0:T(8,128)(2,1)S(1)} %fusion.25), channel_id=1, source_target_pairs={{0,1},{1,2},{2,3},{3,4},{4,5},{5,6},{6,7},{7,0},{8,9},{9,10},{10,1... | collective-permute-start | bytes 786440 | tf_op jit(solution)/shard_map/ppermute | solution.py:15
  91.8 6.7 %collective-permute-start.15 = (bf16[256,512]{1,0:T(8,128)(2,1)S(1)}, bf16[256,512]{1,0:T(8,128)(2,1)S(1)}, u32[]{:S(2)}, u32[]{:S(2)}) collective-permute-start(bf16[256,512]{1,0:T(8,128)(2,1)S(1)} %fusion.27), channel_id=1, source_target_pairs={{0,7},{1,0},{2,1},{3,2},{4,3},{5,4},{6,5},{7,6},{8,15},{9,8},{10,9... | collective-permute-start | bytes 786440 | tf_op jit(solution)/shard_map/ppermute | solution.py:15
  98.0 7.9 %collective-permute-start.12 = (bf16[256,512]{1,0:T(8,128)(2,1)S(1)}, bf16[256,512]{1,0:T(8,128)(2,1)S(1)}, u32[]{:S(2)}, u32[]{:S(2)}) collective-permute-start(bf16[256,512]{1,0:T(8,128)(2,1)S(1)} %fusion.24), channel_id=1, source_target_pairs={{0,1},{1,2},{2,3},{3,4},{4,5},{5,6},{6,7},{7,0},{8,9},{9,10},{10,1... | collective-permute-start | bytes 786440 | tf_op jit(solution)/shard_map/ppermute | solution.py:15
  98.8 8.0 %collective-permute-start.16 = (bf16[256,512]{1,0:T(8,128)(2,1)S(1)}, bf16[256,512]{1,0:T(8,128)(2,1)S(1)}, u32[]{:S(2)}, u32[]{:S(2)}) collective-permute-start(bf16[256,512]{1,0:T(8,128)(2,1)S(1)} %fusion.26), channel_id=1, source_target_pairs={{0,7},{1,0},{2,1},{3,2},{4,3},{5,4},{6,5},{7,6},{8,15},{9,8},{10,9... | collective-permute-start | bytes 786440 | tf_op jit(solution)/shard_map/ppermute | solution.py:15
  106.3 9.1 %collective-permute-start.13 = (bf16[256,512]{1,0:T(8,128)(2,1)S(1)}, bf16[256,512]{1,0:T(8,128)(2,1)S(1)}, u32[]{:S(2)}, u32[]{:S(2)}) collective-permute-start(bf16[256,512]{1,0:T(8,128)(2,1)S(1)} %fusion.23), channel_id=1, source_target_pairs={{0,1},{1,2},{2,3},{3,4},{4,5},{5,6},{6,7},{7,0},{8,9},{9,10},{10,1... | collective-permute-start | bytes 786440 | tf_op jit(solution)/shard_map/ppermute | solution.py:15
  116.4 23.7 %all-to-all-start.1 = ((bf16[16,16,512]{2,1,0:T(8,128)(2,1)}), bf16[16,16,512]{2,1,0:T(8,128)(2,1)S(1)}, u32[]{:S(2)}, u32[]{:S(2)}) async-start(bf16[16,16,512]{2,1,0:T(8,128)(2,1)} %bitcast.7), calls=%async_computation.1 | async-start | bytes 524288 | tf_op jit(solution)/shard_map/all_to_all | solution.py:112
where the time goes:
time: 141 us
  waiting for transfers between devices  56.3 us (40%)
  starting transfers between devices  53.2 us (38%)
  matrix products  23.2 us (16%)
  Pallas kernels  4.69 us (3%)
  other arithmetic  1.98 us (1%)
    all_to_all x2, starting transfers between devices, exchange(): return lax.all_to_all(value, ('column', 'half'), 0, 0, tiled=True)  35.5 us
    ppermute x17, waiting for transfers between devices, shift(): lax.ppermute(value, axis, [(i, (i + by) % size) for i in range(size)])  34.6 us
    all_to_all x2, waiting for transfers between devices, exchange(): return lax.all_to_all(value, ('column', 'half'), 0, 0, tiled=True)  21.7 us
    ppermute x17, starting transfers between devices, shift(): lax.ppermute(value, axis, [(i, (i + by) % size) for i in range(size)])  17.7 us
    dot_general x16, matrix products, accumulate(): jnp.dot(scaled, up, preferred_element_type=f32)  8.38 us
    dot_general x16, matrix products, accumulate(): jnp.dot(scaled, gate, preferred_element_type=f32)  7.24 us
    dot_general x16, matrix products, partial(): jnp.dot(h, block_of(down, owner, w, 1), preferred_element_type=f32)  5.65 us
    pallas_call x1, Pallas kernels, hold_on_chip(): pl.pallas_call(kernel, out_shape=[pltpu.VMEM(a.shape, a.dtype) for a in a...  4.69 us
  transfers between devices with their start and end apart: 19, of which 11 were waited for; matrix products, arithmetic and copies ran while one was open for 12% of the time, Pallas kernels for 0%

commit v1 on v0

--- a/solution.py
+++ b/solution.py
@@ -7,7 +7,6 @@
 
 
 EXPERTS = 8
-CHUNKS = 1
 
 
 def shift(value, axis, by):
@@ -41,42 +40,66 @@
     return lax.dynamic_slice_in_dim(value, index * size, size, axis)
 
 
-def gather_features(chunks, use):
-    n = lax.axis_size("tensor")
-    me = lax.axis_index("tensor")
-    right, left = list(chunks), list(chunks)
-    for i, chunk in enumerate(chunks):
-        use(i, chunk, me)
-    for step in range(1, n // 2 + 1):
-        for i in range(len(chunks)):
-            right[i] = shift(right[i], "tensor", 1)
-            if step < n - n // 2:
-                left[i] = shift(left[i], "tensor", -1)
-            use(i, right[i], (me - step) % n)
-            if step < n - n // 2:
-                use(i, left[i], (me + step) % n)
+class Pairs:
+    def __init__(self):
+        self.size, self.halves = lax.axis_size("tensor"), lax.axis_size("half")
+        self.turn = lax.axis_index("half") % 2
+        self.place = (lax.axis_index("tensor") + self.turn) % self.size
+        self.steps = self.size // 2
+
+    def partner(self, place, step):
+        if step % 2:
+            return place ^ 1
+        return (place + (1 if place % 2 else -1)) % self.size
+
+    def swap(self, value, step):
+        n = self.size
+        route = [
+            (h * n + y, h * n + (self.partner((y + h % 2) % n, step) - h % 2) % n)
+            for h in range(self.halves)
+            for y in range(n)
+        ]
+        return lax.ppermute(value, ("half", "tensor"), route)
+
+    def owners(self, step):
+        base = self.place - self.place % 2
+        away = 2 * (step // 2) * (-1) ** (step + 1)
+        base = base + jnp.where(self.place % 2 == 0, away, -away)
+        return [(base + k - self.turn) % self.size for k in range(2)]
 
 
-def sum_features(make, count):
-    n = lax.axis_size("tensor")
+def gather_features(chunk, use):
+    pairs = Pairs()
+    odd = pairs.place % 2 == 1
+    use(chunk, lax.axis_index("tensor"))
+    other = pairs.swap(chunk, 1)
+    first, second = pairs.owners(1)
+    use(other, jnp.where(odd, first, second))
+    latest = jnp.where(odd, jnp.stack([other, chunk]), jnp.stack([chunk, other]))
+    for step in range(2, pairs.steps + 1):
+        latest = pairs.swap(latest, step)
+        for k, owner in enumerate(pairs.owners(step)):
+            use(latest[k], owner)
+
+
+def sum_features(make):
+    pairs = Pairs()
+    f32, bf16 = jnp.float32, jnp.bfloat16
+    came = None
+    for step in range(pairs.steps, 1, -1):
+        values = lax.optimization_barrier([make(owner) for owner in pairs.owners(step)])
+        if came is not None:
+            values = [value + came[k].astype(f32) for k, value in enumerate(values)]
+        sent = jnp.stack([value.astype(bf16) for value in values])
+        came = pairs.swap(sent, step)
     me = lax.axis_index("tensor")
-    right, left = [None] * count, [None] * count
-    far = n // 2
-    for step in range(far):
-        for i in range(count):
-            value = make(i, (me + far - step) % n)
-            if right[i] is not None:
-                value = value + right[i].astype(jnp.float32)
-            right[i] = shift(value.astype(jnp.bfloat16), "tensor", 1)
-            if step < n - 1 - far:
-                value = make(i, (me - (n - 1 - far - step)) % n)
-                if left[i] is not None:
-                    value = value + left[i].astype(jnp.float32)
-                left[i] = shift(value.astype(jnp.bfloat16), "tensor", -1)
-    return [
-        make(i, me) + right[i].astype(jnp.float32) + left[i].astype(jnp.float32)
-        for i in range(count)
-    ]
+    odd = pairs.place % 2 == 1
+    first, second = pairs.owners(1)
+    mine, other = lax.optimization_barrier((make(me), make(jnp.where(odd, first, second))))
+    mine = mine + jnp.where(odd, came[1], came[0]).astype(f32)
+    other = other + jnp.where(odd, came[0], came[1]).astype(f32)
+    other = pairs.swap(other.astype(bf16), 1)
+    return mine + other.astype(f32)
 
 
 def per_device(tokens, norm_gain, w_gate, w_up, w_down, expert_ids, gate_weights):
@@ -112,39 +135,30 @@
         return lax.all_to_all(value, ("column", "half"), 0, 0, tiled=True)
 
     arrived = exchange(packed).reshape(columns * halves * share, w)
-    rows = arrived.shape[0] // CHUNKS
-    gate_sums = [[0.0] * halves for _ in range(CHUNKS)]
-    up_sums = [[0.0] * halves for _ in range(CHUNKS)]
-    squares = [0.0] * CHUNKS
+    gate_sums, up_sums, squares = [0.0] * halves, [0.0] * halves, [0.0]
 
-    def accumulate(i, block, owner):
+    def accumulate(block, owner):
         values = block.astype(f32)
-        squares[i] = squares[i] + jnp.sum(values * values, axis=1, keepdims=True)
+        squares[0] = squares[0] + jnp.sum(values * values, axis=1, keepdims=True)
         scaled = (values * block_of(norm_gain, owner, w, 0)[None, :]).astype(bf16)
         for k in range(halves):
             gate, up = block_of(gates[k], owner, w, 0), block_of(ups[k], owner, w, 0)
-            gate_sums[i][k] = gate_sums[i][k] + jnp.dot(scaled, gate, preferred_element_type=f32)
-            up_sums[i][k] = up_sums[i][k] + jnp.dot(scaled, up, preferred_element_type=f32)
+            gate_sums[k] = gate_sums[k] + jnp.dot(scaled, gate, preferred_element_type=f32)
+            up_sums[k] = up_sums[k] + jnp.dot(scaled, up, preferred_element_type=f32)
 
-    gather_features([arrived[i * rows : (i + 1) * rows] for i in range(CHUNKS)], accumulate)
-    hidden = []
-    for i in range(CHUNKS):
-        scale = lax.rsqrt(squares[i] / width + 1e-05)
-        hidden.append(
-            [
-                (jax.nn.silu(g * scale) * (u * scale)).astype(bf16)
-                for g, u in zip(gate_sums[i], up_sums[i])
-            ]
+    gather_features(arrived, accumulate)
+    scale = lax.rsqrt(squares[0] / width + 1e-05)
+    hidden = [
+        (jax.nn.silu(g * scale) * (u * scale)).astype(bf16) for g, u in zip(gate_sums, up_sums)
+    ]
+
+    def partial(owner):
+        return sum(
+            jnp.dot(h, block_of(down, owner, w, 1), preferred_element_type=f32)
+            for h, down in zip(hidden, downs)
         )
 
-    def partial(i, owner):
-        return sum(
-            jnp.dot(h, block_of(down, owner, w, 1), preferred_element_type=f32)
-            for h, down in zip(hidden[i], downs)
-        )
-
-    summed = sum_features(partial, CHUNKS)
-    summed = jnp.concatenate(summed, axis=0).astype(bf16)
+    summed = sum_features(partial).astype(bf16)
     returned = exchange(summed.reshape(columns * halves, share, w))
     returned = returned.reshape(EXPERTS * slots, w)
     mix = (select * weight.T[:, None, :]).reshape(EXPERTS * slots, tok_rows)
@@ -177,6 +191,4 @@
         P(rows, None),
     )
 
-    return jax.shard_map(
-        per_device, mesh=inner, in_specs=in_specs, out_specs=P(rows, "tensor"), check_vma=False
-    )
+    return jax.shard_map(per_device, mesh=inner, in_specs=in_specs, out_specs=P(rows, "tensor"), check_vma=False)

time: 141 us -> 153 us (1.085)
  waiting for transfers between devices: 56.3 us -> 78.2 us
  starting transfers between devices: 53.2 us -> 41.4 us
    ppermute x0 -> x8, waiting for transfers between devices: none -> 56.9 us  [swap(): return lax.ppermute(value, ('half', 'tensor'), route)]
    ppermute x17 -> x3, waiting for transfers between devices: 34.6 us -> 0.01 us  [shift(): lax.ppermute(value, axis, [(i, (i + by) % size) for i in range(size)])]
    ppermute x17 -> x3, starting transfers between devices: 17.7 us -> 1.28 us  [shift(): lax.ppermute(value, axis, [(i, (i + by) % size) for i in range(size)])]
    all_to_all x2, starting transfers between devices: 35.5 us -> 39.4 us  [exchange(): return lax.all_to_all(value, ('column', 'half'), 0, 0, tiled=True)]
  transfers between devices with their start and end apart: 19 -> 13, of which waited for: 11 -> 10; matrix products, arithmetic and copies ran while one was open for 12% -> 11% of each run, Pallas kernels for 0% -> 0%
where the time goes in v1:
time: 153 us
  waiting for transfers between devices  78.2 us (51%)
  starting transfers between devices  41.4 us (27%)
  matrix products  22.7 us (15%)
  Pallas kernels  4.69 us (3%)
  other arithmetic  3.24 us (2%)
  local copies, waits for them, and re-layouts  1.9 us (1%)
    ppermute x8, waiting for transfers between devices, swap(): return lax.ppermute(value, ('half', 'tensor'), route)  56.9 us
    all_to_all x2, starting transfers between devices, exchange(): return lax.all_to_all(value, ('column', 'half'), 0, 0, tiled=True)  39.4 us
    all_to_all x2, waiting for transfers between devices, exchange(): return lax.all_to_all(value, ('column', 'half'), 0, 0, tiled=True)  21.3 us
    dot_general x16, matrix products, accumulate(): up_sums[k] = up_sums[k] + jnp.dot(scaled, up, preferred_element_type=f32)  8.65 us
    dot_general x16, matrix products, accumulate(): jnp.dot(scaled, gate, preferred_element_type=f32)  7.19 us
    dot_general x16, matrix products, partial(): jnp.dot(h, block_of(down, owner, w, 1), preferred_element_type=f32)  4.94 us
    pallas_call x1, Pallas kernels, hold_on_chip(): pl.pallas_call(kernel, out_shape=[pltpu.VMEM(a.shape, a.dtype) for a in a...  4.69 us
  transfers between devices with their start and end apart: 13, of which 10 were waited for; matrix products, arithmetic and copies ran while one was open for 11% of the time, Pallas kernels for 0%

profile of v1, /device:TPU:513, one launch (start us, length us, event | category | flops | bytes accessed | tf_op | source)
XLA Modules:
  0.0 152.8 jit_solution(7468077311463152882)
XLA Ops:
  0.0 0.7 convert_reduce_fusion
  1.1 0.9 convolution_convert_fusion
  2.0 23.7 %all-to-all-start = ((bf16[16,16,512]{2,1,0:T(8,128)(2,1)}), bf16[16,16,512]{2,1,0:T(8,128)(2,1)S(1)}, u32[]{:S(2)}, u32[]{:S(2)}) async-start(bf16[16,16,512]{2,1,0:T(8,128)(2,1)} %bitcast.5), calls=%async_computation | async-start | bytes 524288 | tf_op jit(solution)/shard_map/all_to_all | solution.py:135
  25.7 0.8 collective-permute-start.4
  26.7 0.4 collective-permute-start.6
  27.0 0.9 fusion.196
  27.9 9.8 %all-to-all-done = bf16[16,16,512]{2,1,0:T(8,128)(2,1)S(1)} async-done(((bf16[16,16,512]{2,1,0:T(8,128)(2,1)}), bf16[16,16,512]{2,1,0:T(8,128)(2,1)S(1)}, u32[]{:S(2)}, u32[]{:S(2)}) %all-to-all-start) | async-done | bytes 262176 | tf_op jit(solution)/shard_map/all_to_all | solution.py:135
  37.7 1.3 fusion.111
  39.3 1.5 fusion.102
  40.8 3.4 %collective-permute-done = bf16[256,512]{1,0:T(8,128)(2,1)S(1)} collective-permute-done((bf16[256,512]{1,0:T(8,128)(2,1)S(1)}, bf16[256,512]{1,0:T(8,128)(2,1)S(1)}, u32[]{:S(2)}, u32[]{:S(2)}) %collective-permute-start) | collective-permute-done | bytes 262176 | tf_op jit(solution)/shard_map/ppermute | solution.py:62
  44.5 1.3 convolution_add_fusion.23
  45.9 1.5 convolution_add_fusion.16
  47.4 5.3 %collective-permute-done.1 = bf16[2,256,512]{2,1,0:T(8,128)(2,1)S(1)} collective-permute-done((bf16[2,256,512]{2,1,0:T(8,128)(2,1)S(1)}, bf16[2,256,512]{2,1,0:T(8,128)(2,1)S(1)}, u32[]{:S(2)}, u32[]{:S(2)}) %collective-permute-start.1) | collective-permute-done | bytes 524320 | tf_op jit(solution)/shard_map/ppermute | solution.py:62
  52.7 0.3 convolution_add_fusion.22
  53.0 1.3 convolution_add_fusion.15
  54.4 0.3 convolution_add_fusion.21
  54.9 0.3 convolution_add_fusion.14
  55.2 6.7 %collective-permute-done.2 = bf16[2,256,512]{2,1,0:T(8,128)(2,1)S(1)} collective-permute-done((bf16[2,256,512]{2,1,0:T(8,128)(2,1)S(1)}, bf16[2,256,512]{2,1,0:T(8,128)(2,1)S(1)}, u32[]{:S(2)}, u32[]{:S(2)}) %collective-permute-start.2) | collective-permute-done | bytes 524320 | tf_op jit(solution)/shard_map/ppermute | solution.py:62
  61.9 0.3 convolution_add_fusion.20
  62.2 0.3 convolution_add_fusion.13
  62.7 0.3 convolution_add_fusion.19
  63.1 0.3 convolution_add_fusion.12
  63.4 6.9 %collective-permute-done.3 = bf16[2,256,512]{2,1,0:T(8,128)(2,1)S(1)} collective-permute-done((bf16[2,256,512]{2,1,0:T(8,128)(2,1)S(1)}, bf16[2,256,512]{2,1,0:T(8,128)(2,1)S(1)}, u32[]{:S(2)}, u32[]{:S(2)}) %collective-permute-start.3) | collective-permute-done | bytes 524320 | tf_op jit(solution)/shard_map/ppermute | solution.py:62
  70.5 0.3 convolution_add_fusion.18
  70.8 0.3 convolution_add_fusion.11
  71.1 0.3 fusion.17
  71.4 0.4 fusion.18
  71.8 0.8 copy-done.3
  72.9 0.3 fusion.45
  73.9 0.3 fusion.54
  74.2 4.7 %shard_map.73 = (bf16[4096,512]{1,0:T(8,128)(2,1)S(1)}, bf16[4096,512]{1,0:T(8,128)(2,1)S(1)}, bf16[512,4096]{1,0:T(8,128)(2,1)S(1)}) custom-call(bf16[4096,512]{1,0:T(8,128)(2,1)} %collective-permute-done.4.refs_0_, bf16[4096,512]{1,0:T(8,128)(2,1)} %collective-permute-done.5.refs_1_, bf16[512,4096]{1,0:T(8,128)(2,1)} %collective-permute-done.6.refs_2_), custom_call_target="tpu_custom_call" | custom-call | tf_op jit(solution)/shard_map/pallas_call | solution.py:29
  78.9 0.3 fusion.80
  79.3 0.3 fusion.78
  79.6 0.3 fusion.84
  79.9 0.3 fusion.82
  80.2 0.3 fusion.88
  80.5 0.3 fusion.86
  80.8 0.3 fusion.90
  81.2 0.4 fusion.14
  81.6 0.3 fusion.65
  81.9 0.3 fusion.63
  82.3 0.3 fusion.69
  82.6 0.3 fusion.67
  82.9 0.3 fusion.73
  83.2 0.3 fusion.71
  83.5 0.3 fusion.75
  83.8 0.5 fusion.19
  84.4 0.3 convolution_add_fusion
  84.7 0.3 convolution_add_fusion.1
  85.2 0.3 fusion.57
  85.5 0.3 convolution_add_fusion.2
  85.8 0.3 convolution_add_fusion.3
  86.2 7.3 %collective-permute-done.7 = bf16[2,256,512]{2,1,0:T(8,128)(2,1)S(1)} collective-permute-done((bf16[2,256,512]{2,1,0:T(8,128)(2,1)S(1)}, bf16[2,256,512]{2,1,0:T(8,128)(2,1)S(1)}, u32[]{:S(2)}, u32[]{:S(2)}) %collective-permute-start.7) | collective-permute-done | bytes 524320 | tf_op jit(solution)/shard_map/ppermute | solution.py:62
  94.2 0.3 convolution_add_fusion.4
  94.5 0.3 convolution_add_fusion.5
  94.8 8.9 %collective-permute-done.8 = bf16[2,256,512]{2,1,0:T(8,128)(2,1)S(1)} collective-permute-done((bf16[2,256,512]{2,1,0:T(8,128)(2,1)S(1)}, bf16[2,256,512]{2,1,0:T(8,128)(2,1)S(1)}, u32[]{:S(2)}, u32[]{:S(2)}) %collective-permute-start.8) | collective-permute-done | bytes 524320 | tf_op jit(solution)/shard_map/ppermute | solution.py:62
  104.5 0.3 convolution_add_fusion.6
  104.8 0.3 convolution_add_fusion.7
  105.1 8.9 %collective-permute-done.9 = bf16[2,256,512]{2,1,0:T(8,128)(2,1)S(1)} collective-permute-done((bf16[2,256,512]{2,1,0:T(8,128)(2,1)S(1)}, bf16[2,256,512]{2,1,0:T(8,128)(2,1)S(1)}, u32[]{:S(2)}, u32[]{:S(2)}) %collective-permute-start.9) | collective-permute-done | bytes 524320 | tf_op jit(solution)/shard_map/ppermute | solution.py:62
  114.2 9.5 %collective-permute-done.10 = bf16[256,512]{1,0:T(8,128)(2,1)S(1)} collective-permute-done((bf16[256,512]{1,0:T(8,128)(2,1)S(1)}, bf16[256,512]{1,0:T(8,128)(2,1)S(1)}, u32[]{:S(2)}, u32[]{:S(2)}) %collective-permute-start.10) | collective-permute-done | bytes 262176 | tf_op jit(solution)/shard_map/ppermute | solution.py:62
  123.8 0.8 fusion.36
  124.6 15.7 %all-to-all-start.1 = ((bf16[16,16,512]{2,1,0:T(8,128)(2,1)}), bf16[16,16,512]{2,1,0:T(8,128)(2,1)S(1)}, u32[]{:S(2)}, u32[]{:S(2)}) async-start(bf16[16,16,512]{2,1,0:T(8,128)(2,1)} %bitcast.33), calls=%async_computation.1 | async-start | bytes 524288 | tf_op jit(solution)/shard_map/all_to_all | solution.py:135
  140.3 11.5 %all-to-all-done.1 = bf16[16,16,512]{2,1,0:T(8,128)(2,1)S(1)} async-done(((bf16[16,16,512]{2,1,0:T(8,128)(2,1)}), bf16[16,16,512]{2,1,0:T(8,128)(2,1)S(1)}, u32[]{:S(2)}, u32[]{:S(2)}) %all-to-all-start.1) | async-done | bytes 262176 | tf_op jit(solution)/shard_map/all_to_all | solution.py:135
  151.8 0.9 convolution_convert_fusion.1
  (46 shorter events, 4.4 us)
Async XLA Ops:
  0.0 1.1 copy-start
  2.0 35.7 %all-to-all-start = ((bf16[16,16,512]{2,1,0:T(8,128)(2,1)}), bf16[16,16,512]{2,1,0:T(8,128)(2,1)S(1)}, u32[]{:S(2)}, u32[]{:S(2)}) async-start(bf16[16,16,512]{2,1,0:T(8,128)(2,1)} %bitcast.5), calls=%async_computation | async-start | bytes 524288 | tf_op jit(solution)/shard_map/all_to_all | solution.py:135
  25.7 48.5 %collective-permute-start.4 = (bf16[4096,512]{1,0:T(8,128)(2,1)}, bf16[4096,512]{1,0:T(8,128)(2,1)}, u32[]{:S(2)}, u32[]{:S(2)}) collective-permute-start(bf16[4096,512]{1,0:T(8,128)(2,1)} %param.9), channel_id=1, source_target_pairs={{0,8},{8,0},{1,9},{9,1},{2,10},{10,2},{3,11},{11,3},{4,12},{12,4},... | collective-permute-start | bytes 12582920 | tf_op jit(solution)/shard_map/ppermute | solution.py:14
  26.5 47.7 %collective-permute-start.5 = (bf16[4096,512]{1,0:T(8,128)(2,1)}, bf16[4096,512]{1,0:T(8,128)(2,1)}, u32[]{:S(2)}, u32[]{:S(2)}) collective-permute-start(bf16[4096,512]{1,0:T(8,128)(2,1)} %param.10), channel_id=1, source_target_pairs={{0,8},{8,0},{1,9},{9,1},{2,10},{10,2},{3,11},{11,3},{4,12},{12,4},... | collective-permute-start | bytes 12582920 | tf_op jit(solution)/shard_map/ppermute | solution.py:14
  26.7 47.6 %collective-permute-start.6 = (bf16[512,4096]{1,0:T(8,128)(2,1)}, bf16[512,4096]{1,0:T(8,128)(2,1)}, u32[]{:S(2)}, u32[]{:S(2)}) collective-permute-start(bf16[512,4096]{1,0:T(8,128)(2,1)} %param.11), channel_id=1, source_target_pairs={{0,8},{8,0},{1,9},{9,1},{2,10},{10,2},{3,11},{11,3},{4,12},{12,4},... | collective-permute-start | bytes 12582920 | tf_op jit(solution)/shard_map/ppermute | solution.py:14
  37.7 6.4 %collective-permute-start = (bf16[256,512]{1,0:T(8,128)(2,1)S(1)}, bf16[256,512]{1,0:T(8,128)(2,1)S(1)}, u32[]{:S(2)}, u32[]{:S(2)}) collective-permute-start(bf16[256,512]{1,0:T(8,128)(2,1)S(1)} %bitcast.143), channel_id=1, source_target_pairs={{0,1},{1,0},{2,3},{3,2},{4,5},{5,4},{6,7},{7,6},{8,15},{9,10},{10,... | collective-permute-start | bytes 786440 | tf_op jit(solution)/shard_map/ppermute | solution.py:62
  39.3 13.4 %copy-start.2 = (bf16[4096,512]{1,0:T(8,128)(2,1)S(1)}, bf16[4096,512]{1,0:T(8,128)(2,1)}, u32[]{:S(2)}) copy-start(bf16[4096,512]{1,0:T(8,128)(2,1)} %param.9) | copy-start | bytes 12582916
  44.2 8.4 %collective-permute-start.1 = (bf16[2,256,512]{2,1,0:T(8,128)(2,1)S(1)}, bf16[2,256,512]{2,1,0:T(8,128)(2,1)S(1)}, u32[]{:S(2)}, u32[]{:S(2)}) collective-permute-start(bf16[2,256,512]{2,1,0:T(8,128)(2,1)S(1)} %maximum_select_fusion), channel_id=1, source_target_pairs={{0,7},{1,2},{2,1},{3,4},{4,3},{5,6},{6,5},{7,0},{8,9},{9,8},{10,11... | collective-permute-start | bytes 1572872 | tf_op jit(solution)/shard_map/ppermute | solution.py:62
  45.9 9.0 %copy-start.4 = (bf16[4096,512]{1,0:T(8,128)(2,1)S(1)}, bf16[4096,512]{1,0:T(8,128)(2,1)}, u32[]{:S(2)}) copy-start(bf16[4096,512]{1,0:T(8,128)(2,1)} %param.10) | copy-start | bytes 12582916
  52.7 9.2 %collective-permute-start.2 = (bf16[2,256,512]{2,1,0:T(8,128)(2,1)S(1)}, bf16[2,256,512]{2,1,0:T(8,128)(2,1)S(1)}, u32[]{:S(2)}, u32[]{:S(2)}) collective-permute-start(bf16[2,256,512]{2,1,0:T(8,128)(2,1)S(1)} %collective-permute-done.1), channel_id=1, source_target_pairs={{0,1},{1,0},{2,3},{3,2},{4,5},{5,4},{6,7},{7,6},{8,15},{9,10},{10,... | collective-permute-start | bytes 1572872 | tf_op jit(solution)/shard_map/ppermute | solution.py:62
  61.9 8.3 %collective-permute-start.3 = (bf16[2,256,512]{2,1,0:T(8,128)(2,1)S(1)}, bf16[2,256,512]{2,1,0:T(8,128)(2,1)S(1)}, u32[]{:S(2)}, u32[]{:S(2)}) collective-permute-start(bf16[2,256,512]{2,1,0:T(8,128)(2,1)S(1)} %collective-permute-done.2), channel_id=1, source_target_pairs={{0,7},{1,2},{2,1},{3,4},{4,3},{5,6},{6,5},{7,0},{8,9},{9,8},{10,11... | collective-permute-start | bytes 1572872 | tf_op jit(solution)/shard_map/ppermute | solution.py:62
  70.4 2.2 %copy-start.3 = (bf16[512,4096]{1,0:T(8,128)(2,1)S(1)}, bf16[512,4096]{1,0:T(8,128)(2,1)}, u32[]{:S(2)}) copy-start(bf16[512,4096]{1,0:T(8,128)(2,1)} %param.11) | copy-start | bytes 12582916
  85.1 8.4 %collective-permute-start.7 = (bf16[2,256,512]{2,1,0:T(8,128)(2,1)S(1)}, bf16[2,256,512]{2,1,0:T(8,128)(2,1)S(1)}, u32[]{:S(2)}, u32[]{:S(2)}) collective-permute-start(bf16[2,256,512]{2,1,0:T(8,128)(2,1)S(1)} %pad_maximum_fusion), channel_id=1, source_target_pairs={{0,7},{1,2},{2,1},{3,4},{4,3},{5,6},{6,5},{7,0},{8,9},{9,8},{10,11... | collective-permute-start | bytes 1572872 | tf_op jit(solution)/shard_map/ppermute | solution.py:62
  93.7 10.0 %collective-permute-start.8 = (bf16[2,256,512]{2,1,0:T(8,128)(2,1)S(1)}, bf16[2,256,512]{2,1,0:T(8,128)(2,1)S(1)}, u32[]{:S(2)}, u32[]{:S(2)}) collective-permute-start(bf16[2,256,512]{2,1,0:T(8,128)(2,1)S(1)} %pad_maximum_fusion.1), channel_id=1, source_target_pairs={{0,1},{1,0},{2,3},{3,2},{4,5},{5,4},{6,7},{7,6},{8,15},{9,10},{10,... | collective-permute-start | bytes 1572872 | tf_op jit(solution)/shard_map/ppermute | solution.py:62
  103.9 48.8 %copy-start.1 = (bf16[64,512]{1,0:T(8,128)(2,1)S(1)}, bf16[64,512]{1,0:T(8,128)(2,1)}, u32[]{:S(2)}) copy-start(bf16[64,512]{1,0:T(8,128)(2,1)} %param.7) | copy-start | bytes 196612
  104.0 10.0 %collective-permute-start.9 = (bf16[2,256,512]{2,1,0:T(8,128)(2,1)S(1)}, bf16[2,256,512]{2,1,0:T(8,128)(2,1)S(1)}, u32[]{:S(2)}, u32[]{:S(2)}) collective-permute-start(bf16[2,256,512]{2,1,0:T(8,128)(2,1)S(1)} %pad_maximum_fusion.2), channel_id=1, source_target_pairs={{0,7},{1,2},{2,1},{3,4},{4,3},{5,6},{6,5},{7,0},{8,9},{9,8},{10,11... | collective-permute-start | bytes 1572872 | tf_op jit(solution)/shard_map/ppermute | solution.py:62
  114.1 9.7 %collective-permute-start.10 = (bf16[256,512]{1,0:T(8,128)(2,1)S(1)}, bf16[256,512]{1,0:T(8,128)(2,1)S(1)}, u32[]{:S(2)}, u32[]{:S(2)}) collective-permute-start(bf16[256,512]{1,0:T(8,128)(2,1)S(1)} %fusion.34), channel_id=1, source_target_pairs={{0,1},{1,0},{2,3},{3,2},{4,5},{5,4},{6,7},{7,6},{8,15},{9,10},{10,... | collective-permute-start | bytes 786440 | tf_op jit(solution)/shard_map/ppermute | solution.py:62
  124.6 27.3 %all-to-all-start.1 = ((bf16[16,16,512]{2,1,0:T(8,128)(2,1)}), bf16[16,16,512]{2,1,0:T(8,128)(2,1)S(1)}, u32[]{:S(2)}, u32[]{:S(2)}) async-start(bf16[16,16,512]{2,1,0:T(8,128)(2,1)} %bitcast.33), calls=%async_computation.1 | async-start | bytes 524288 | tf_op jit(solution)/shard_map/all_to_all | solution.py:135
